TPU v7x, 32 devices: a whole 2x2x4 slice. The times are simulated.
32 devices in a mesh: groups: 2 (over y), blk: 4 (over z), cols: 2 (over x), sub: 2 (over core).
Axes of the slice: x: 2, y: 2, z: 4, core: 2. Of those that a mesh axis runs over, the one named last changes fastest.
Arguments:
- features: bfloat16 [4096, 256], P(('groups', 'blk', 'cols'), 'sub'), parts along dimension 0, may hold values from -60 to 60, as said below
- vector: float32 [4096], P(('groups', 'blk', 'cols')), parts along dimension 0, may hold values from 0.1 to 100, as said below
Outputs:
- new_vector: float32 [4096], P(('groups', 'blk', 'cols')), parts along dimension 0
- mean_affinity: float32 [4096], P(('groups', 'blk', 'cols')), parts along dimension 0
There are 2 independent parts, one for each index of `groups`. A program takes and returns all parts, laid end to end along the dimension named above; each array names one. Nothing has to cross between parts.
Inputs may be any that keep to these rules, and one draw needn't show every extreme that they name: Real-valued features; no row is zero. `vector`: positive entries.
All inputs are finite; a program needn't handle non-finite values. Where the computation divides by a largest or mean magnitude, that divisor is 1e-20 or more.
Results may differ from a plain program's by a relative error of at most 0.0033.
Values may be sent and summed in bfloat16 or wider, within the bound.
No kernel may reach another device: no remote copies, remote signals or barrier semaphores. Data moves between devices by JAX's collectives and lax.ppermute only.
A program may use at most 64 MiB of HBM per device.

v0:
```python
import functools
import math

import jax
import jax.numpy as jnp
from jax import lax
from jax.experimental import pallas as pl
from jax.experimental.pallas import tpu as pltpu
from jax.sharding import PartitionSpec as P

POWER = 16
AXES = ("blk", "cols", "sub")
PAD = 16
BULKS = 1
WIDE = 256
TALL = 256
DEPTH = 3
LATE = 3
EACH = ((1, 0, 0), (0, 1, 0))
VMEM = pl.BlockSpec(memory_space=pltpu.VMEM)
HBM = pl.BlockSpec(memory_space=pltpu.HBM)


def power(base):
    for _ in range(POWER.bit_length() - 1):
        base = base * base
    return base


def fold_block(row_feats, totals, col_feats, col_vals):
    cosine = lax.dot_general(
        row_feats, col_feats, (((1,), (1,)), ((), ())), preferred_element_type=jnp.float32
    )
    affinity = power((1.0 + cosine) * 0.5)
    weighted = totals[0] + jnp.dot(affinity, col_vals, precision=lax.Precision.HIGHEST)
    degree = totals[1] + jnp.sum(affinity, axis=1)
    return (weighted, degree)


def sweep(row_feats, totals, pieces):
    col_feats, col_vals = pieces
    columns = col_feats.shape[0]
    block_len = math.gcd(columns, 512)
    blocks = columns // block_len
    if blocks == 1:
        return fold_block(row_feats, totals, col_feats, col_vals)
    stacked = (
        col_feats.reshape(blocks, block_len, col_feats.shape[1]),
        col_vals.reshape(blocks, block_len),
    )

    def advance(running, member):
        return (fold_block(row_feats, running, member[0], member[1]), None)

    result, _ = lax.scan(advance, totals, stacked)
    return result


def reduced(features, vector):
    own_rows = features.shape[0]
    half_rows = own_rows // 2
    gathered = lax.all_gather(features, "sub", axis=1, tiled=True)
    widened = gathered.astype(jnp.float32)
    unit_rows = (
        widened
        * lax.rsqrt(jnp.mean(widened * widened, axis=1, keepdims=True) + 1e-06)
        * (1.0 / math.sqrt(widened.shape[1]))
    ).astype(jnp.bfloat16)
    sub_index = lax.axis_index("sub")
    col_feats = lax.dynamic_slice_in_dim(unit_rows, sub_index * half_rows, half_rows, 0)
    col_vals = lax.dynamic_slice_in_dim(vector, sub_index * half_rows, half_rows, 0)
    points = own_rows * lax.axis_size("blk") * lax.axis_size("cols")
    block_feats = lax.all_gather(unit_rows, "cols", axis=0, tiled=True)
    zeros = jnp.zeros((block_feats.shape[0],), jnp.float32)
    partial_sums = sweep(
        block_feats,
        (zeros, zeros),
        (
            lax.all_gather(col_feats, "blk", axis=0, tiled=True),
            lax.all_gather(col_vals.astype(jnp.bfloat16), "blk", axis=0, tiled=True).astype(
                jnp.float32
            ),
        ),
    )
    block_weighted, block_degree = lax.psum((partial_sums[0], partial_sums[1]), ("cols", "sub"))
    block_averaged = block_weighted / block_degree
    total = lax.psum(jnp.sum(jnp.abs(block_averaged)), "blk")
    first_row = lax.axis_index("cols") * own_rows
    averaged = lax.dynamic_slice_in_dim(block_averaged, first_row, own_rows, 0)
    degree = lax.dynamic_slice_in_dim(block_degree, first_row, own_rows, 0)
    mean_abs = total / points + 1e-06
    return (averaged / mean_abs, degree / points)


def swap(x, *masks):
    sizes = [lax.axis_size(axis) for axis in AXES]
    place = lambda b, c, s: (b * sizes[1] + c) * sizes[2] + s
    pairs = [
        (place(b, c, s), place(*(at ^ mask for at, mask in zip((b, c, s), masks[s % len(masks)]))))
        for b in range(sizes[0])
        for c in range(sizes[1])
        for s in range(sizes[2])
    ]
    return lax.ppermute(x, AXES, pairs)


def pack(features, vector, packed, row, sems):
    rows = features.shape[0]
    size = rows // BULKS
    bulk = [
        pltpu.make_async_copy(
            features.at[k * size : (k + 1) * size], packed.at[k * size : (k + 1) * size], sems.at[k]
        )
        for k in range(BULKS)
    ]
    line = pltpu.make_async_copy(vector, row, sems.at[BULKS])
    line.start()
    for copy in bulk:
        copy.start()
    line.wait()
    value = row[...]
    high = value.astype(jnp.bfloat16)
    low = (value - high.astype(jnp.float32)).astype(jnp.bfloat16)
    rest = jnp.zeros((PAD - 2 * row.shape[0], row.shape[1]), jnp.bfloat16)
    packed[rows : rows + PAD, :] = jnp.concatenate([high, low, rest])
    for copy in bulk:
        copy.wait()


def admit(mine, base, theirs, twin, rows, unit, weights, at):
    half = mine.shape[1]
    width = 2 * half
    lines = rows // half
    a = mine[base : base + rows, :].astype(jnp.float32)
    b = theirs[twin : twin + rows, :].astype(jnp.float32)
    scale = lax.rsqrt(jnp.sum(a * a + b * b, axis=1, keepdims=True) / width + 1e-06)
    scale = scale * (1.0 / math.sqrt(width))
    unit[at : at + rows, :half] = (a * scale).astype(jnp.bfloat16)
    unit[at : at + rows, half:] = (b * scale).astype(jnp.bfloat16)
    tail = mine[base + rows : base + rows + PAD, :].astype(jnp.float32)
    for line in range(lines):
        span = slice(at + line * half, at + (line + 1) * half)
        weights[0:1, span] = tail[line : line + 1, :]
        weights[1:2, span] = tail[lines + line : lines + line + 1, :]
    ones = lax.broadcasted_iota(jnp.int32, (6, rows), 0) == 0
    weights[2:8, at : at + rows] = jnp.where(ones, 1.0, 0.0)


def product(left, right):
    return lax.dot_general(
        left, right, (((1,), (1,)), ((), ())), preferred_element_type=jnp.float32
    )


def step(rows, olds, slots, last, *refs):
    refs = list(refs)
    old = [refs[3 * k : 3 * k + 3] for k in range(olds)]
    count = 1 + max(max(i, j) for i, base, j, twin in slots)
    given, outs = refs[3 * olds : 3 * olds + count], refs[3 * olds + count :]
    if last:
        new_ref, mean_ref, unit, weights, results, sems = outs
        sums, old_sums = None, None
    else:
        unit, weights, sums = outs[:3]
        old_sums = outs[3:]
    fresh = 0
    for i, base, j, twin in slots:
        admit(given[i], base * (rows + PAD), given[j], twin * (rows + PAD), rows, unit, weights, fresh)
        fresh += rows
    names = [block[0] for block in old] + [unit]
    lines = [block[1][...].astype(jnp.bfloat16) for block in old] + [weights[...].astype(jnp.bfloat16)]
    here = len(old)
    tiles = []
    for k, block in enumerate(old):
        size = block[0].shape[0]
        for j in range(0, size, WIDE):
            tiles += [
                (at, min(at + TALL, fresh), k, j, min(j + WIDE, size)) for at in range(0, fresh, TALL)
            ]
    for at in range(0, fresh, rows):
        tiles += [(at, at + rows, here, j, min(j + WIDE, at)) for j in range(0, at, WIDE)]
        tiles += [(at, at + rows, here, at, at + rows)]
    columns, along, cosines, affinities = {}, {}, [], []

    def fold(table, key, value):
        table[key] = table[key] + value if key in table else value

    def add(tile, value):
        at, stop, k, j, end = tile
        found = jnp.dot(lines[here][:, at:stop], value, preferred_element_type=jnp.float32)
        for c in range(j, end, rows):
            fold(columns, (k, c), found[:, c - j : c - j + rows])
        if (k, j) != (here, at):
            found = product(value, lines[k][:, j:end])
            for r in range(at, stop, rows):
                fold(along, r, found[r - at : r - at + rows, :])

    for tile in tiles + [None] * (DEPTH + LATE + 2):
        if tile:
            at, stop, k, j, end = tile
            cosines.append((tile, product(unit[at:stop, :], names[k][j:end, :])))
        if cosines and (len(cosines) > DEPTH or not tile):
            done, value = cosines.pop(0)
            affinities.append((done, power(1.0 + value).astype(jnp.bfloat16)))
        if affinities and (len(affinities) > LATE or not (tile or cosines)):
            add(*affinities.pop(0))
    assert not cosines and not affinities
    for at, value in along.items():
        fold(columns, (here, at), value.T)

    def joined(k, size):
        return jnp.concatenate([columns[k, c] for c in range(0, size, rows)], axis=1)

    totals = [block[2][...] + joined(k, block[0].shape[0]) for k, block in enumerate(old)]
    total = joined(here, fresh)
    if not last:
        sums[...] = total
        for ref, value in zip(old_sums, totals):
            ref[...] = value
        return
    points = fresh + sum(block[0].shape[0] for block in old)
    leave = [
        pltpu.make_async_copy(results.at[k : k + 1], ref, sems.at[k])
        for k, ref in enumerate((new_ref, mean_ref))
    ]
    results[1:2, :] = totals[0][2:3, :rows] * (0.5**POWER / points)
    leave[1].start()
    averaged = [(t[0:1] + t[1:2]) / t[2:3] for t in totals + [total]]
    mean_abs = sum(jnp.sum(jnp.abs(a)) for a in averaged) / points + 1e-06
    results[0:1, :] = averaged[0][:, :rows] / mean_abs
    leave[0].start()
    for copy in leave:
        copy.wait()


def gathered(features, vector):
    rows, half = features.shape
    lines = rows // half
    shape = jax.ShapeDtypeStruct
    far_blk = lax.axis_size("blk") // 2
    params = pltpu.CompilerParams(vmem_limit_bytes=24 * 2**20)

    def advance(blocks, given, slots, last=False):
        fresh = len(slots) * rows
        unit, weights = shape((fresh, 2 * half), jnp.bfloat16), shape((8, fresh), jnp.float32)
        done = sum(block[0].shape[0] for block in blocks)
        outs = [unit, weights, weights] + [shape(block[2].shape, jnp.float32) for block in blocks]
        scratch = []
        if last:
            outs = [shape((1, rows), jnp.float32)] * 2
            scratch = [pltpu.VMEM(x.shape, x.dtype) for x in (unit, weights)]
            scratch += [pltpu.VMEM((2, rows), jnp.float32), pltpu.SemaphoreType.DMA((2,))]
        inputs = [x for block in blocks for x in block] + given
        work = 2 * 2 * half * fresh * (fresh + done)
        result = pl.pallas_call(
            functools.partial(step, rows, len(blocks), slots, last),
            out_shape=outs,
            in_specs=[VMEM] * len(inputs),
            out_specs=[HBM if last else VMEM] * len(outs),
            scratch_shapes=scratch,
            compiler_params=params,
            cost_estimate=pl.CostEstimate(flops=work, bytes_accessed=0, transcendentals=0),
        )(*inputs)
        if last:
            return result
        return [(b[0], b[1], s) for b, s in zip(blocks, result[3:])] + [tuple(result[:3])]

    place = pltpu.with_memory_space_constraint
    own = pl.pallas_call(
        pack,
        out_shape=pltpu.VMEM((rows + PAD, half), jnp.bfloat16),
        in_specs=[HBM, HBM],
        out_specs=VMEM,
        scratch_shapes=[pltpu.VMEM((lines, half), jnp.float32), pltpu.SemaphoreType.DMA((BULKS + 1,))],
        compiler_params=params,
        name="pack",
    )(place(features, pltpu.HBM), place(vector.reshape(lines, half), pltpu.HBM))
    other, both, each = (0, 0, 1), (1, 1, 0), EACH
    far = swap(own, (far_blk, 0, 0))
    own2 = swap(own, other)
    dn = swap(own, both)
    na = swap(jnp.concatenate([own, own2]), *each)
    far2 = swap(far, other)
    df = swap(far, both)
    fa = swap(jnp.concatenate([far, far2]), *each)
    dn2 = swap(dn, other)
    na2 = swap(na, other)
    df2 = swap(df, other)
    fa2 = swap(fa, other)
    blocks = advance([], [own, own2, far, far2], [(0, 0, 1, 0), (2, 0, 3, 0)])
    blocks = advance(blocks, [na, dn, dn2], [(0, 0, 0, 1), (1, 0, 2, 0)])
    blocks = advance(blocks, [na2], [(0, 1, 0, 0)])
    blocks = advance(blocks, [df, df2, fa], [(0, 0, 1, 0), (2, 0, 2, 1)])
    new, mean = advance(blocks, [fa2], [(0, 1, 0, 0)], True)
    return new.reshape(rows), mean.reshape(rows)


def solution(mesh):
    in_specs = (P(("groups", "blk", "cols"), "sub"), P(("groups", "blk", "cols")))
    out_specs = (P(("groups", "blk", "cols")), P(("groups", "blk", "cols")))
    few = (mesh.shape["blk"], mesh.shape["cols"], mesh.shape["sub"]) == (4, 2, 2)
    return jax.shard_map(
        gathered if few else reduced,
        mesh=mesh,
        in_specs=in_specs,
        out_specs=out_specs,
        check_vma=False,
    )
```

profile of v0, /device:TPU:0, one launch (start us, length us, event | category | flops | bytes accessed | tf_op | source)
XLA Modules:
  0.0 25.5 jit_solution(4042553916083147867)
XLA Ops:
  0.6 0.9 %pack.1.refs_0_ = bf16[272,128]{1,0:T(8,128)(2,1)S(1)} custom-call(bf16[256,128]{1,0:T(8,128)(2,1)} %features.1, f32[2,128]{1,0:T(2,128)} %bitcast.3), custom_call_target="tpu_custom_call" | custom-call | tf_op jit(solution)/shard_map/pack/pallas_call | solution.py:269
  1.5 4.1 %collective-permute-start.1 = (bf16[272,128]{1,0:T(8,128)(2,1)S(1)}, bf16[272,128]{1,0:T(8,128)(2,1)S(1)}, u32[]{:S(2)}, u32[]{:S(2)}) collective-permute-start(bf16[272,128]{1,0:T(8,128)(2,1)S(1)} %pack.1.refs_0_), channel_id=1, source_target_pairs={{0,8},{1,9},{2,10},{3,11},{4,12},{5,13},{6,14},{7,15},{8,0},{9,1},... | collective-permute-start | bytes 208904 | tf_op jit(solution)/shard_map/ppermute | solution.py:104
  5.6 0.0 collective-permute-start
  5.6 3.8 %collective-permute-done.1.refs_2_ = bf16[272,128]{1,0:T(8,128)(2,1)S(1)} collective-permute-done((bf16[272,128]{1,0:T(8,128)(2,1)S(1)}, bf16[272,128]{1,0:T(8,128)(2,1)S(1)}, u32[]{:S(2)}, u32[]{:S(2)}) %collective-permute-start.1) | collective-permute-done | bytes 69664 | tf_op jit(solution)/shard_map/ppermute | solution.py:104
  9.4 0.0 collective-permute-start.2
  9.4 0.0 collective-permute-done.refs_1_
  9.4 0.7 %collective-permute-start.3 = (bf16[544,128]{1,0:T(8,128)(2,1)S(1)}, bf16[544,128]{1,0:T(8,128)(2,1)S(1)}, u32[]{:S(2)}, u32[]{:S(2)}) collective-permute-start(bf16[544,128]{1,0:T(8,128)(2,1)S(1)} %pad_maximum_fusion), channel_id=1, source_target_pairs={{0,4},{1,3},{2,6},{3,1},{4,0},{5,7},{6,2},{7,5},{8,12},{9,11},{10,... | collective-permute-start | bytes 417800 | tf_op jit(solution)/shard_map/ppermute | solution.py:104
  10.1 0.6 %collective-permute-done.2.refs_3_ = bf16[272,128]{1,0:T(8,128)(2,1)S(1)} collective-permute-done((bf16[272,128]{1,0:T(8,128)(2,1)S(1)}, bf16[272,128]{1,0:T(8,128)(2,1)S(1)}, u32[]{:S(2)}, u32[]{:S(2)}) %collective-permute-start.2) | collective-permute-done | bytes 69664 | tf_op jit(solution)/shard_map/ppermute | solution.py:104
  10.7 0.9 %collective-permute-start.9 = (bf16[544,128]{1,0:T(8,128)(2,1)S(1)}, bf16[544,128]{1,0:T(8,128)(2,1)S(1)}, u32[]{:S(2)}, u32[]{:S(2)}) collective-permute-start(bf16[544,128]{1,0:T(8,128)(2,1)S(1)} %pad_maximum_fusion.1), channel_id=1, source_target_pairs={{0,4},{1,3},{2,6},{3,1},{4,0},{5,7},{6,2},{7,5},{8,12},{9,11},{10,... | collective-permute-start | bytes 417800 | tf_op jit(solution)/shard_map/ppermute | solution.py:104
  11.6 2.3 %collective-permute-start.4 = (bf16[272,128]{1,0:T(8,128)(2,1)S(1)}, bf16[272,128]{1,0:T(8,128)(2,1)S(1)}, u32[]{:S(2)}, u32[]{:S(2)}) collective-permute-start(bf16[272,128]{1,0:T(8,128)(2,1)S(1)} %pack.1.refs_0_), channel_id=1, source_target_pairs={{0,6},{1,7},{2,4},{3,5},{4,2},{5,3},{6,0},{7,1},{8,14},{9,15},{10,... | collective-permute-start | bytes 208904 | tf_op jit(solution)/shard_map/ppermute | solution.py:104
  13.9 0.6 %collective-permute-done.3.refs_3_ = bf16[544,128]{1,0:T(8,128)(2,1)S(1)} collective-permute-done((bf16[544,128]{1,0:T(8,128)(2,1)S(1)}, bf16[544,128]{1,0:T(8,128)(2,1)S(1)}, u32[]{:S(2)}, u32[]{:S(2)}) %collective-permute-start.3) | collective-permute-done | bytes 139296 | tf_op jit(solution)/shard_map/ppermute | solution.py:104
  14.6 0.0 collective-permute-start.6
  14.6 1.5 %collective-permute-start.7 = (bf16[272,128]{1,0:T(8,128)(2,1)S(1)}, bf16[272,128]{1,0:T(8,128)(2,1)S(1)}, u32[]{:S(2)}, u32[]{:S(2)}) collective-permute-start(bf16[272,128]{1,0:T(8,128)(2,1)S(1)} %collective-permute-done.1.refs_2_), channel_id=1, source_target_pairs={{0,6},{1,7},{2,4},{3,5},{4,2},{5,3},{6,0},{7,1},{8,14},{9,15},{10,... | collective-permute-start | bytes 208904 | tf_op jit(solution)/shard_map/ppermute | solution.py:104
  16.1 2.7 %collective-permute-done.4.refs_4_ = bf16[272,128]{1,0:T(8,128)(2,1)S(1)} collective-permute-done((bf16[272,128]{1,0:T(8,128)(2,1)S(1)}, bf16[272,128]{1,0:T(8,128)(2,1)S(1)}, u32[]{:S(2)}, u32[]{:S(2)}) %collective-permute-start.4) | collective-permute-done | bytes 69664 | tf_op jit(solution)/shard_map/ppermute | solution.py:104
  18.8 0.0 collective-permute-start.5
  18.8 0.0 collective-permute-done.9.refs_11_
  18.8 0.5 %collective-permute-start.10 = (bf16[544,128]{1,0:T(8,128)(2,1)S(1)}, bf16[544,128]{1,0:T(8,128)(2,1)S(1)}, u32[]{:S(2)}, u32[]{:S(2)}) collective-permute-start(bf16[544,128]{1,0:T(8,128)(2,1)S(1)} %collective-permute-done.9.refs_11_), channel_id=1, source_target_pairs={{0,1},{1,0},{2,3},{3,2},{4,5},{5,4},{6,7},{7,6},{8,9},{9,8},{10,11... | collective-permute-start | bytes 417800 | tf_op jit(solution)/shard_map/ppermute | solution.py:104
  19.3 0.9 %collective-permute-done.7.refs_9_ = bf16[272,128]{1,0:T(8,128)(2,1)S(1)} collective-permute-done((bf16[272,128]{1,0:T(8,128)(2,1)S(1)}, bf16[272,128]{1,0:T(8,128)(2,1)S(1)}, u32[]{:S(2)}, u32[]{:S(2)}) %collective-permute-start.7) | collective-permute-done | bytes 69664 | tf_op jit(solution)/shard_map/ppermute | solution.py:104
  20.2 0.0 collective-permute-start.8
  20.2 0.7 %shard_map.41 = (bf16[512,256]{1,0:T(8,128)(2,1)S(1)}, f32[8,512]{1,0:T(8,128)S(1)}, f32[8,512]{1,0:T(8,128)S(1)}) custom-call(bf16[272,128]{1,0:T(8,128)(2,1)S(1)} %pack.1.refs_0_, bf16[272,128]{1,0:T(8,128)(2,1)S(1)} %collective-permute-done.refs_1_, bf16[272,128]{1,0:T(8,128)(2,1)S(1)} %collective-permute-done.1.refs_2_, ...), custom_call_target="tpu_custom_call" | custom-call | flops 134217728 | tf_op jit(solution)/shard_map/pallas_call | solution.py:255
  20.8 0.0 collective-permute-done.5.refs_5_
  20.8 0.9 %shard_map.42 = (bf16[512,256]{1,0:T(8,128)(2,1)S(1)}, f32[8,512]{1,0:T(8,128)S(1)}, f32[8,512]{1,0:T(8,128)S(1)}, f32[8,512]{1,0:T(8,128)S(1)}) custom-call(bf16[512,256]{1,0:T(8,128)(2,1)S(1)} %get-tuple-element.22.refs_0_, f32[8,512]{1,0:T(8,128)S(1)} %get-tuple-element.23.refs_1_, f32[8,512]{1,0:T(8,128)S(1)} %get-tuple-element.24.refs_2_, ...), custom_call_target="tpu_custom_call" | custom-call | flops 268435456 | tf_op jit(solution)/shard_map/pallas_call | solution.py:255
  21.7 0.0 collective-permute-done.6.refs_6_
  21.7 0.8 %shard_map.43 = (bf16[256,256]{1,0:T(8,128)(2,1)S(1)}, f32[8,256]{1,0:T(8,128)S(1)}, f32[8,256]{1,0:T(8,128)S(1)}, f32[8,512]{1,0:T(8,128)S(1)}, f32[8,512]{1,0:T(8,128)S(1)}) custom-call(bf16[512,256]{1,0:T(8,128)(2,1)S(1)} %get-tuple-element.22.refs_0_, f32[8,512]{1,0:T(8,128)S(1)} %get-tuple-element.23.refs_1_, f32[8,512]{1,0:T(8,128)S(1)} %get-tuple-element.25.refs_2_, ...), custom_call_target="tpu_custom_call" | custom-call | flops 167772160 | tf_op jit(solution)/shard_map/pallas_call | solution.py:255
  22.5 0.0 collective-permute-done.8.refs_10_
  22.5 1.3 %shard_map.44 = (bf16[512,256]{1,0:T(8,128)(2,1)S(1)}, f32[8,512]{1,0:T(8,128)S(1)}, f32[8,512]{1,0:T(8,128)S(1)}, f32[8,512]{1,0:T(8,128)S(1)}, f32[8,512]{1,0:T(8,128)S(1)}, /*index=5*/f32[8,256]{1,0:T(8,128)S(1)}) custom-call(bf16[512,256]{1,0:T(8,128)(2,1)S(1)} %get-tuple-element.22.refs_0_, f32[8,512]{1,0:T(8,128)S(1)} %get-tuple-element.23.refs_1_, ...), custom_call_target="tpu_custom_call" | custom-call | flops 469762048 | tf_op jit(solution)/shard_map/pallas_call | solution.py:255
  23.8 0.0 collective-permute-done.10.refs_12_
  23.9 1.7 %shard_map.45 = (f32[1,256]{1,0:T(1,128)}, f32[1,256]{1,0:T(1,128)}) custom-call(bf16[512,256]{1,0:T(8,128)(2,1)S(1)} %get-tuple-element.22.refs_0_, f32[8,512]{1,0:T(8,128)S(1)} %get-tuple-element.23.refs_1_, f32[8,512]{1,0:T(8,128)S(1)} %get-tuple-element.34.refs_2_, bf16[512,256]{1,0:T(8,128)(2,1)S(1)} %get-tuple-element.26.refs_3_, ...), custom_call_target="tpu_custom_call" | custom-call | flops 268435456 | tf_op jit(solution)/shard_map/pallas_call | solution.py:255
  (2 shorter events, 0.0 us)
Async XLA Ops:
  1.5 7.9 %collective-permute-start.1 = (bf16[272,128]{1,0:T(8,128)(2,1)S(1)}, bf16[272,128]{1,0:T(8,128)(2,1)S(1)}, u32[]{:S(2)}, u32[]{:S(2)}) collective-permute-start(bf16[272,128]{1,0:T(8,128)(2,1)S(1)} %pack.1.refs_0_), channel_id=1, source_target_pairs={{0,8},{1,9},{2,10},{3,11},{4,12},{5,13},{6,14},{7,15},{8,0},{9,1},... | collective-permute-start | bytes 208904 | tf_op jit(solution)/shard_map/ppermute | solution.py:104
  5.6 3.8 %collective-permute-start = (bf16[272,128]{1,0:T(8,128)(2,1)S(1)}, bf16[272,128]{1,0:T(8,128)(2,1)S(1)}, u32[]{:S(2)}, u32[]{:S(2)}) collective-permute-start(bf16[272,128]{1,0:T(8,128)(2,1)S(1)} %pack.1.refs_0_), channel_id=1, source_target_pairs={{0,1},{1,0},{2,3},{3,2},{4,5},{5,4},{6,7},{7,6},{8,9},{9,8},{10,11... | collective-permute-start | bytes 208904 | tf_op jit(solution)/shard_map/ppermute | solution.py:104
  9.4 1.3 %collective-permute-start.2 = (bf16[272,128]{1,0:T(8,128)(2,1)S(1)}, bf16[272,128]{1,0:T(8,128)(2,1)S(1)}, u32[]{:S(2)}, u32[]{:S(2)}) collective-permute-start(bf16[272,128]{1,0:T(8,128)(2,1)S(1)} %collective-permute-done.1.refs_2_), channel_id=1, source_target_pairs={{0,1},{1,0},{2,3},{3,2},{4,5},{5,4},{6,7},{7,6},{8,9},{9,8},{10,11... | collective-permute-start | bytes 208904 | tf_op jit(solution)/shard_map/ppermute | solution.py:104
  9.4 5.1 %collective-permute-start.3 = (bf16[544,128]{1,0:T(8,128)(2,1)S(1)}, bf16[544,128]{1,0:T(8,128)(2,1)S(1)}, u32[]{:S(2)}, u32[]{:S(2)}) collective-permute-start(bf16[544,128]{1,0:T(8,128)(2,1)S(1)} %pad_maximum_fusion), channel_id=1, source_target_pairs={{0,4},{1,3},{2,6},{3,1},{4,0},{5,7},{6,2},{7,5},{8,12},{9,11},{10,... | collective-permute-start | bytes 417800 | tf_op jit(solution)/shard_map/ppermute | solution.py:104
  10.7 8.1 %collective-permute-start.9 = (bf16[544,128]{1,0:T(8,128)(2,1)S(1)}, bf16[544,128]{1,0:T(8,128)(2,1)S(1)}, u32[]{:S(2)}, u32[]{:S(2)}) collective-permute-start(bf16[544,128]{1,0:T(8,128)(2,1)S(1)} %pad_maximum_fusion.1), channel_id=1, source_target_pairs={{0,4},{1,3},{2,6},{3,1},{4,0},{5,7},{6,2},{7,5},{8,12},{9,11},{10,... | collective-permute-start | bytes 417800 | tf_op jit(solution)/shard_map/ppermute | solution.py:104
  11.6 7.2 %collective-permute-start.4 = (bf16[272,128]{1,0:T(8,128)(2,1)S(1)}, bf16[272,128]{1,0:T(8,128)(2,1)S(1)}, u32[]{:S(2)}, u32[]{:S(2)}) collective-permute-start(bf16[272,128]{1,0:T(8,128)(2,1)S(1)} %pack.1.refs_0_), channel_id=1, source_target_pairs={{0,6},{1,7},{2,4},{3,5},{4,2},{5,3},{6,0},{7,1},{8,14},{9,15},{10,... | collective-permute-start | bytes 208904 | tf_op jit(solution)/shard_map/ppermute | solution.py:104
  14.6 7.1 %collective-permute-start.6 = (bf16[544,128]{1,0:T(8,128)(2,1)S(1)}, bf16[544,128]{1,0:T(8,128)(2,1)S(1)}, u32[]{:S(2)}, u32[]{:S(2)}) collective-permute-start(bf16[544,128]{1,0:T(8,128)(2,1)S(1)} %collective-permute-done.3.refs_3_), channel_id=1, source_target_pairs={{0,1},{1,0},{2,3},{3,2},{4,5},{5,4},{6,7},{7,6},{8,9},{9,8},{10,11... | collective-permute-start | bytes 417800 | tf_op jit(solution)/shard_map/ppermute | solution.py:104
  14.6 5.6 %collective-permute-start.7 = (bf16[272,128]{1,0:T(8,128)(2,1)S(1)}, bf16[272,128]{1,0:T(8,128)(2,1)S(1)}, u32[]{:S(2)}, u32[]{:S(2)}) collective-permute-start(bf16[272,128]{1,0:T(8,128)(2,1)S(1)} %collective-permute-done.1.refs_2_), channel_id=1, source_target_pairs={{0,6},{1,7},{2,4},{3,5},{4,2},{5,3},{6,0},{7,1},{8,14},{9,15},{10,... | collective-permute-start | bytes 208904 | tf_op jit(solution)/shard_map/ppermute | solution.py:104
  18.8 2.0 %collective-permute-start.5 = (bf16[272,128]{1,0:T(8,128)(2,1)S(1)}, bf16[272,128]{1,0:T(8,128)(2,1)S(1)}, u32[]{:S(2)}, u32[]{:S(2)}) collective-permute-start(bf16[272,128]{1,0:T(8,128)(2,1)S(1)} %collective-permute-done.4.refs_4_), channel_id=1, source_target_pairs={{0,1},{1,0},{2,3},{3,2},{4,5},{5,4},{6,7},{7,6},{8,9},{9,8},{10,11... | collective-permute-start | bytes 208904 | tf_op jit(solution)/shard_map/ppermute | solution.py:104
  18.8 5.0 %collective-permute-start.10 = (bf16[544,128]{1,0:T(8,128)(2,1)S(1)}, bf16[544,128]{1,0:T(8,128)(2,1)S(1)}, u32[]{:S(2)}, u32[]{:S(2)}) collective-permute-start(bf16[544,128]{1,0:T(8,128)(2,1)S(1)} %collective-permute-done.9.refs_11_), channel_id=1, source_target_pairs={{0,1},{1,0},{2,3},{3,2},{4,5},{5,4},{6,7},{7,6},{8,9},{9,8},{10,11... | collective-permute-start | bytes 417800 | tf_op jit(solution)/shard_map/ppermute | solution.py:104
  20.2 2.3 %collective-permute-start.8 = (bf16[272,128]{1,0:T(8,128)(2,1)S(1)}, bf16[272,128]{1,0:T(8,128)(2,1)S(1)}, u32[]{:S(2)}, u32[]{:S(2)}) collective-permute-start(bf16[272,128]{1,0:T(8,128)(2,1)S(1)} %collective-permute-done.7.refs_9_), channel_id=1, source_target_pairs={{0,1},{1,0},{2,3},{3,2},{4,5},{5,4},{6,7},{7,6},{8,9},{9,8},{10,11... | collective-permute-start | bytes 208904 | tf_op jit(solution)/shard_map/ppermute | solution.py:104
where the time goes:
time: 25.7 us; the launch traced here: 25.5 us
  starting transfers between devices  10.1 us (39%)
  waiting for transfers between devices  8.55 us (33%)
  Pallas kernels  6.21 us (24%)
  between operations  0.66 us (3%)
    ppermute x11, starting transfers between devices, swap(): return lax.ppermute(x, AXES, pairs)  10.1 us
    ppermute x11, waiting for transfers between devices, swap(): return lax.ppermute(x, AXES, pairs)  8.55 us
    pallas_call x5, Pallas kernels, advance(): pl.pallas_call(functools.partial(step, rows, len(blocks), slots, last), o...  5.34 us
    pallas_call x1, Pallas kernels, gathered(): pl.pallas_call(pack, out_shape=pltpu.VMEM((rows + PAD, half), jnp.bfloat1...  0.87 us
  transfers between devices with their start and end apart: 11, of which 5 were waited for; matrix products, arithmetic and copies ran while one was open for 0% of the time, Pallas kernels for 14%

commit v1 on v0

--- a/solution.py
+++ b/solution.py
@@ -10,12 +10,12 @@
 
 POWER = 16
 AXES = ("blk", "cols", "sub")
-PAD = 16
+PAD = 8
 BULKS = 1
 WIDE = 256
 TALL = 256
-DEPTH = 3
-LATE = 3
+DEPTH = 20
+LATE = 20
 EACH = ((1, 0, 0), (0, 1, 0))
 VMEM = pl.BlockSpec(memory_space=pltpu.VMEM)
 HBM = pl.BlockSpec(memory_space=pltpu.HBM)

time: 25.7 us -> 25.5 us (level)
  no operation moved by 1% of the time
where the time goes in v1:
time: 25.5 us; the launch traced here: 25.3 us
  starting transfers between devices  10 us (39%)
  waiting for transfers between devices  8.35 us (33%)
  Pallas kernels  6.22 us (24%)
  between operations  0.66 us (3%)
    ppermute x11, starting transfers between devices, swap(): return lax.ppermute(x, AXES, pairs)  10 us
    ppermute x11, waiting for transfers between devices, swap(): return lax.ppermute(x, AXES, pairs)  8.35 us
    pallas_call x5, Pallas kernels, advance(): pl.pallas_call(functools.partial(step, rows, len(blocks), slots, last), o...  5.35 us
    pallas_call x1, Pallas kernels, gathered(): pl.pallas_call(pack, out_shape=pltpu.VMEM((rows + PAD, half), jnp.bfloat1...  0.87 us
  transfers between devices with their start and end apart: 11, of which 5 were waited for; matrix products, arithmetic and copies ran while one was open for 0% of the time, Pallas kernels for 14%

profile of v1, /device:TPU:0, one launch (start us, length us, event | category | flops | bytes accessed | tf_op | source)
XLA Modules:
  0.0 25.3 jit_solution(7081248219588565582)
XLA Ops:
  0.6 0.9 %pack.1.refs_0_ = bf16[264,128]{1,0:T(8,128)(2,1)S(1)} custom-call(bf16[256,128]{1,0:T(8,128)(2,1)} %features.1, f32[2,128]{1,0:T(2,128)} %bitcast.3), custom_call_target="tpu_custom_call" | custom-call | tf_op jit(solution)/shard_map/pack/pallas_call | solution.py:269
  1.5 4.1 %collective-permute-start.1 = (bf16[264,128]{1,0:T(8,128)(2,1)S(1)}, bf16[264,128]{1,0:T(8,128)(2,1)S(1)}, u32[]{:S(2)}, u32[]{:S(2)}) collective-permute-start(bf16[264,128]{1,0:T(8,128)(2,1)S(1)} %pack.1.refs_0_), channel_id=1, source_target_pairs={{0,8},{1,9},{2,10},{3,11},{4,12},{5,13},{6,14},{7,15},{8,0},{9,1},... | collective-permute-start | bytes 202760 | tf_op jit(solution)/shard_map/ppermute | solution.py:104
  5.6 0.0 collective-permute-start
  5.6 3.7 %collective-permute-done.1.refs_2_ = bf16[264,128]{1,0:T(8,128)(2,1)S(1)} collective-permute-done((bf16[264,128]{1,0:T(8,128)(2,1)S(1)}, bf16[264,128]{1,0:T(8,128)(2,1)S(1)}, u32[]{:S(2)}, u32[]{:S(2)}) %collective-permute-start.1) | collective-permute-done | bytes 67616 | tf_op jit(solution)/shard_map/ppermute | solution.py:104
  9.4 0.0 collective-permute-start.2
  9.4 0.0 collective-permute-done.refs_1_
  9.4 0.7 %collective-permute-start.3 = (bf16[528,128]{1,0:T(8,128)(2,1)S(1)}, bf16[528,128]{1,0:T(8,128)(2,1)S(1)}, u32[]{:S(2)}, u32[]{:S(2)}) collective-permute-start(bf16[528,128]{1,0:T(8,128)(2,1)S(1)} %pad_maximum_fusion), channel_id=1, source_target_pairs={{0,4},{1,3},{2,6},{3,1},{4,0},{5,7},{6,2},{7,5},{8,12},{9,11},{10,... | collective-permute-start | bytes 405512 | tf_op jit(solution)/shard_map/ppermute | solution.py:104
  10.0 0.6 %collective-permute-done.2.refs_3_ = bf16[264,128]{1,0:T(8,128)(2,1)S(1)} collective-permute-done((bf16[264,128]{1,0:T(8,128)(2,1)S(1)}, bf16[264,128]{1,0:T(8,128)(2,1)S(1)}, u32[]{:S(2)}, u32[]{:S(2)}) %collective-permute-start.2) | collective-permute-done | bytes 67616 | tf_op jit(solution)/shard_map/ppermute | solution.py:104
  10.6 0.9 %collective-permute-start.9 = (bf16[528,128]{1,0:T(8,128)(2,1)S(1)}, bf16[528,128]{1,0:T(8,128)(2,1)S(1)}, u32[]{:S(2)}, u32[]{:S(2)}) collective-permute-start(bf16[528,128]{1,0:T(8,128)(2,1)S(1)} %pad_maximum_fusion.1), channel_id=1, source_target_pairs={{0,4},{1,3},{2,6},{3,1},{4,0},{5,7},{6,2},{7,5},{8,12},{9,11},{10,... | collective-permute-start | bytes 405512 | tf_op jit(solution)/shard_map/ppermute | solution.py:104
  11.6 2.3 %collective-permute-start.4 = (bf16[264,128]{1,0:T(8,128)(2,1)S(1)}, bf16[264,128]{1,0:T(8,128)(2,1)S(1)}, u32[]{:S(2)}, u32[]{:S(2)}) collective-permute-start(bf16[264,128]{1,0:T(8,128)(2,1)S(1)} %pack.1.refs_0_), channel_id=1, source_target_pairs={{0,6},{1,7},{2,4},{3,5},{4,2},{5,3},{6,0},{7,1},{8,14},{9,15},{10,... | collective-permute-start | bytes 202760 | tf_op jit(solution)/shard_map/ppermute | solution.py:104
  13.9 0.6 %collective-permute-done.3.refs_3_ = bf16[528,128]{1,0:T(8,128)(2,1)S(1)} collective-permute-done((bf16[528,128]{1,0:T(8,128)(2,1)S(1)}, bf16[528,128]{1,0:T(8,128)(2,1)S(1)}, u32[]{:S(2)}, u32[]{:S(2)}) %collective-permute-start.3) | collective-permute-done | bytes 135200 | tf_op jit(solution)/shard_map/ppermute | solution.py:104
  14.5 0.0 collective-permute-start.6
  14.5 1.5 %collective-permute-start.7 = (bf16[264,128]{1,0:T(8,128)(2,1)S(1)}, bf16[264,128]{1,0:T(8,128)(2,1)S(1)}, u32[]{:S(2)}, u32[]{:S(2)}) collective-permute-start(bf16[264,128]{1,0:T(8,128)(2,1)S(1)} %collective-permute-done.1.refs_2_), channel_id=1, source_target_pairs={{0,6},{1,7},{2,4},{3,5},{4,2},{5,3},{6,0},{7,1},{8,14},{9,15},{10,... | collective-permute-start | bytes 202760 | tf_op jit(solution)/shard_map/ppermute | solution.py:104
  16.0 2.5 %collective-permute-done.4.refs_4_ = bf16[264,128]{1,0:T(8,128)(2,1)S(1)} collective-permute-done((bf16[264,128]{1,0:T(8,128)(2,1)S(1)}, bf16[264,128]{1,0:T(8,128)(2,1)S(1)}, u32[]{:S(2)}, u32[]{:S(2)}) %collective-permute-start.4) | collective-permute-done | bytes 67616 | tf_op jit(solution)/shard_map/ppermute | solution.py:104
  18.5 0.0 collective-permute-start.5
  18.5 0.0 collective-permute-done.9.refs_11_
  18.5 0.5 %collective-permute-start.10 = (bf16[528,128]{1,0:T(8,128)(2,1)S(1)}, bf16[528,128]{1,0:T(8,128)(2,1)S(1)}, u32[]{:S(2)}, u32[]{:S(2)}) collective-permute-start(bf16[528,128]{1,0:T(8,128)(2,1)S(1)} %collective-permute-done.9.refs_11_), channel_id=1, source_target_pairs={{0,1},{1,0},{2,3},{3,2},{4,5},{5,4},{6,7},{7,6},{8,9},{9,8},{10,11... | collective-permute-start | bytes 405512 | tf_op jit(solution)/shard_map/ppermute | solution.py:104
  19.0 0.9 %collective-permute-done.7.refs_9_ = bf16[264,128]{1,0:T(8,128)(2,1)S(1)} collective-permute-done((bf16[264,128]{1,0:T(8,128)(2,1)S(1)}, bf16[264,128]{1,0:T(8,128)(2,1)S(1)}, u32[]{:S(2)}, u32[]{:S(2)}) %collective-permute-start.7) | collective-permute-done | bytes 67616 | tf_op jit(solution)/shard_map/ppermute | solution.py:104
  19.9 0.0 collective-permute-start.8
  19.9 0.7 %shard_map.41 = (bf16[512,256]{1,0:T(8,128)(2,1)S(1)}, f32[8,512]{1,0:T(8,128)S(1)}, f32[8,512]{1,0:T(8,128)S(1)}) custom-call(bf16[264,128]{1,0:T(8,128)(2,1)S(1)} %pack.1.refs_0_, bf16[264,128]{1,0:T(8,128)(2,1)S(1)} %collective-permute-done.refs_1_, bf16[264,128]{1,0:T(8,128)(2,1)S(1)} %collective-permute-done.1.refs_2_, ...), custom_call_target="tpu_custom_call" | custom-call | flops 134217728 | tf_op jit(solution)/shard_map/pallas_call | solution.py:255
  20.6 0.0 collective-permute-done.5.refs_5_
  20.6 0.9 %shard_map.42 = (bf16[512,256]{1,0:T(8,128)(2,1)S(1)}, f32[8,512]{1,0:T(8,128)S(1)}, f32[8,512]{1,0:T(8,128)S(1)}, f32[8,512]{1,0:T(8,128)S(1)}) custom-call(bf16[512,256]{1,0:T(8,128)(2,1)S(1)} %get-tuple-element.22.refs_0_, f32[8,512]{1,0:T(8,128)S(1)} %get-tuple-element.23.refs_1_, f32[8,512]{1,0:T(8,128)S(1)} %get-tuple-element.24.refs_2_, ...), custom_call_target="tpu_custom_call" | custom-call | flops 268435456 | tf_op jit(solution)/shard_map/pallas_call | solution.py:255
  21.5 0.0 collective-permute-done.6.refs_6_
  21.5 0.8 %shard_map.43 = (bf16[256,256]{1,0:T(8,128)(2,1)S(1)}, f32[8,256]{1,0:T(8,128)S(1)}, f32[8,256]{1,0:T(8,128)S(1)}, f32[8,512]{1,0:T(8,128)S(1)}, f32[8,512]{1,0:T(8,128)S(1)}) custom-call(bf16[512,256]{1,0:T(8,128)(2,1)S(1)} %get-tuple-element.22.refs_0_, f32[8,512]{1,0:T(8,128)S(1)} %get-tuple-element.23.refs_1_, f32[8,512]{1,0:T(8,128)S(1)} %get-tuple-element.25.refs_2_, ...), custom_call_target="tpu_custom_call" | custom-call | flops 167772160 | tf_op jit(solution)/shard_map/pallas_call | solution.py:255
  22.3 0.0 collective-permute-done.8.refs_10_
  22.3 1.3 %shard_map.44 = (bf16[512,256]{1,0:T(8,128)(2,1)S(1)}, f32[8,512]{1,0:T(8,128)S(1)}, f32[8,512]{1,0:T(8,128)S(1)}, f32[8,512]{1,0:T(8,128)S(1)}, f32[8,512]{1,0:T(8,128)S(1)}, /*index=5*/f32[8,256]{1,0:T(8,128)S(1)}) custom-call(bf16[512,256]{1,0:T(8,128)(2,1)S(1)} %get-tuple-element.22.refs_0_, f32[8,512]{1,0:T(8,128)S(1)} %get-tuple-element.23.refs_1_, ...), custom_call_target="tpu_custom_call" | custom-call | flops 469762048 | tf_op jit(solution)/shard_map/pallas_call | solution.py:255
  23.6 0.0 collective-permute-done.10.refs_12_
  23.6 1.7 %shard_map.45 = (f32[1,256]{1,0:T(1,128)}, f32[1,256]{1,0:T(1,128)}) custom-call(bf16[512,256]{1,0:T(8,128)(2,1)S(1)} %get-tuple-element.22.refs_0_, f32[8,512]{1,0:T(8,128)S(1)} %get-tuple-element.23.refs_1_, f32[8,512]{1,0:T(8,128)S(1)} %get-tuple-element.34.refs_2_, bf16[512,256]{1,0:T(8,128)(2,1)S(1)} %get-tuple-element.26.refs_3_, ...), custom_call_target="tpu_custom_call" | custom-call | flops 268435456 | tf_op jit(solution)/shard_map/pallas_call | solution.py:255
  (2 shorter events, 0.0 us)
Async XLA Ops:
  1.5 7.8 %collective-permute-start.1 = (bf16[264,128]{1,0:T(8,128)(2,1)S(1)}, bf16[264,128]{1,0:T(8,128)(2,1)S(1)}, u32[]{:S(2)}, u32[]{:S(2)}) collective-permute-start(bf16[264,128]{1,0:T(8,128)(2,1)S(1)} %pack.1.refs_0_), channel_id=1, source_target_pairs={{0,8},{1,9},{2,10},{3,11},{4,12},{5,13},{6,14},{7,15},{8,0},{9,1},... | collective-permute-start | bytes 202760 | tf_op jit(solution)/shard_map/ppermute | solution.py:104
  5.6 3.7 %collective-permute-start = (bf16[264,128]{1,0:T(8,128)(2,1)S(1)}, bf16[264,128]{1,0:T(8,128)(2,1)S(1)}, u32[]{:S(2)}, u32[]{:S(2)}) collective-permute-start(bf16[264,128]{1,0:T(8,128)(2,1)S(1)} %pack.1.refs_0_), channel_id=1, source_target_pairs={{0,1},{1,0},{2,3},{3,2},{4,5},{5,4},{6,7},{7,6},{8,9},{9,8},{10,11... | collective-permute-start | bytes 202760 | tf_op jit(solution)/shard_map/ppermute | solution.py:104
  9.4 1.3 %collective-permute-start.2 = (bf16[264,128]{1,0:T(8,128)(2,1)S(1)}, bf16[264,128]{1,0:T(8,128)(2,1)S(1)}, u32[]{:S(2)}, u32[]{:S(2)}) collective-permute-start(bf16[264,128]{1,0:T(8,128)(2,1)S(1)} %collective-permute-done.1.refs_2_), channel_id=1, source_target_pairs={{0,1},{1,0},{2,3},{3,2},{4,5},{5,4},{6,7},{7,6},{8,9},{9,8},{10,11... | collective-permute-start | bytes 202760 | tf_op jit(solution)/shard_map/ppermute | solution.py:104
  9.4 5.1 %collective-permute-start.3 = (bf16[528,128]{1,0:T(8,128)(2,1)S(1)}, bf16[528,128]{1,0:T(8,128)(2,1)S(1)}, u32[]{:S(2)}, u32[]{:S(2)}) collective-permute-start(bf16[528,128]{1,0:T(8,128)(2,1)S(1)} %pad_maximum_fusion), channel_id=1, source_target_pairs={{0,4},{1,3},{2,6},{3,1},{4,0},{5,7},{6,2},{7,5},{8,12},{9,11},{10,... | collective-permute-start | bytes 405512 | tf_op jit(solution)/shard_map/ppermute | solution.py:104
  10.6 7.9 %collective-permute-start.9 = (bf16[528,128]{1,0:T(8,128)(2,1)S(1)}, bf16[528,128]{1,0:T(8,128)(2,1)S(1)}, u32[]{:S(2)}, u32[]{:S(2)}) collective-permute-start(bf16[528,128]{1,0:T(8,128)(2,1)S(1)} %pad_maximum_fusion.1), channel_id=1, source_target_pairs={{0,4},{1,3},{2,6},{3,1},{4,0},{5,7},{6,2},{7,5},{8,12},{9,11},{10,... | collective-permute-start | bytes 405512 | tf_op jit(solution)/shard_map/ppermute | solution.py:104
  11.6 7.0 %collective-permute-start.4 = (bf16[264,128]{1,0:T(8,128)(2,1)S(1)}, bf16[264,128]{1,0:T(8,128)(2,1)S(1)}, u32[]{:S(2)}, u32[]{:S(2)}) collective-permute-start(bf16[264,128]{1,0:T(8,128)(2,1)S(1)} %pack.1.refs_0_), channel_id=1, source_target_pairs={{0,6},{1,7},{2,4},{3,5},{4,2},{5,3},{6,0},{7,1},{8,14},{9,15},{10,... | collective-permute-start | bytes 202760 | tf_op jit(solution)/shard_map/ppermute | solution.py:104
  14.5 7.0 %collective-permute-start.6 = (bf16[528,128]{1,0:T(8,128)(2,1)S(1)}, bf16[528,128]{1,0:T(8,128)(2,1)S(1)}, u32[]{:S(2)}, u32[]{:S(2)}) collective-permute-start(bf16[528,128]{1,0:T(8,128)(2,1)S(1)} %collective-permute-done.3.refs_3_), channel_id=1, source_target_pairs={{0,1},{1,0},{2,3},{3,2},{4,5},{5,4},{6,7},{7,6},{8,9},{9,8},{10,11... | collective-permute-start | bytes 405512 | tf_op jit(solution)/shard_map/ppermute | solution.py:104
  14.5 5.5 %collective-permute-start.7 = (bf16[264,128]{1,0:T(8,128)(2,1)S(1)}, bf16[264,128]{1,0:T(8,128)(2,1)S(1)}, u32[]{:S(2)}, u32[]{:S(2)}) collective-permute-start(bf16[264,128]{1,0:T(8,128)(2,1)S(1)} %collective-permute-done.1.refs_2_), channel_id=1, source_target_pairs={{0,6},{1,7},{2,4},{3,5},{4,2},{5,3},{6,0},{7,1},{8,14},{9,15},{10,... | collective-permute-start | bytes 202760 | tf_op jit(solution)/shard_map/ppermute | solution.py:104
  18.5 2.1 %collective-permute-start.5 = (bf16[264,128]{1,0:T(8,128)(2,1)S(1)}, bf16[264,128]{1,0:T(8,128)(2,1)S(1)}, u32[]{:S(2)}, u32[]{:S(2)}) collective-permute-start(bf16[264,128]{1,0:T(8,128)(2,1)S(1)} %collective-permute-done.4.refs_4_), channel_id=1, source_target_pairs={{0,1},{1,0},{2,3},{3,2},{4,5},{5,4},{6,7},{7,6},{8,9},{9,8},{10,11... | collective-permute-start | bytes 202760 | tf_op jit(solution)/shard_map/ppermute | solution.py:104
  18.5 5.0 %collective-permute-start.10 = (bf16[528,128]{1,0:T(8,128)(2,1)S(1)}, bf16[528,128]{1,0:T(8,128)(2,1)S(1)}, u32[]{:S(2)}, u32[]{:S(2)}) collective-permute-start(bf16[528,128]{1,0:T(8,128)(2,1)S(1)} %collective-permute-done.9.refs_11_), channel_id=1, source_target_pairs={{0,1},{1,0},{2,3},{3,2},{4,5},{5,4},{6,7},{7,6},{8,9},{9,8},{10,11... | collective-permute-start | bytes 405512 | tf_op jit(solution)/shard_map/ppermute | solution.py:104
  19.9 2.3 %collective-permute-start.8 = (bf16[264,128]{1,0:T(8,128)(2,1)S(1)}, bf16[264,128]{1,0:T(8,128)(2,1)S(1)}, u32[]{:S(2)}, u32[]{:S(2)}) collective-permute-start(bf16[264,128]{1,0:T(8,128)(2,1)S(1)} %collective-permute-done.7.refs_9_), channel_id=1, source_target_pairs={{0,1},{1,0},{2,3},{3,2},{4,5},{5,4},{6,7},{7,6},{8,9},{9,8},{10,11... | collective-permute-start | bytes 202760 | tf_op jit(solution)/shard_map/ppermute | solution.py:104
